TPU v7x, 128 devices: a whole 4x4x4 slice. The times are simulated.
128 devices in a mesh: group: 32 (over x, z, core), tensor: 4 (over y).
Axes of the slice: x: 4, y: 4, z: 4, core: 2. Of those that a mesh axis runs over, the one named last changes fastest.
Arguments:
- queries: bfloat16 [4096, 4096], P('group', 'tensor'), may hold values from -120 to 120
- keys: bfloat16 [4096, 512], P('group', 'tensor'), may hold values from -6 to 6
- values: bfloat16 [4096, 512], P('group', 'tensor'), may hold values from -6 to 6
- document_index: int32 [32, 128], P('group'), may hold values from 0 to 7, never falling along the last dimension, each value on 1 to 64 neighbouring positions
- out_proj: bfloat16 [4096, 4096], P('tensor', 'group'), may hold values from -0.25 to 0.25
- residual_in: bfloat16 [4096, 4096], P(('group', 'tensor')), may hold values from -60 to 60
- norm_gain: float32 [4096], replicated, may hold values from 0.1 to 1.9
- expert_ids: int32 [4096, 8], P(('group', 'tensor')), may hold values from 0 to 127, all different within a row; in each aligned block of 32 rows (0 to 31, 32 to 63, ...) at most 4 rows name the same one
- gate_weights: float32 [4096, 8], P(('group', 'tensor')), may hold values from 0.05 to 0.45
- w_gate_up: bfloat16 [128, 4096, 1536], P(('group', 'tensor')), may hold values from -0.09375 to 0.09375
- w_down: bfloat16 [128, 768, 4096], P(('group', 'tensor')), may hold values from -0.21875 to 0.21875
Outputs:
- layer_out: bfloat16 [4096, 4096], P(('group', 'tensor'))
Inputs may be any that keep to these rules, and one draw needn't show every extreme that they name: `document_index`: ids never fall along a group's tokens; equal ids mark one document. `expert_ids`: a token names 8 different experts; among the 32 tokens of one device (aligned blocks of rows) no expert is named more than 4 times, a bound that some block reaches.
All inputs are finite; a program needn't handle non-finite values.
Results may differ from a plain program's by a relative error of at most 0.0045.
Values may be sent and summed in bfloat16 or wider, within the bound.
A program may use at most 128 MiB of HBM per device.

v0:
```python
import jax
import jax.numpy as jnp
from jax import lax
from jax.sharding import PartitionSpec as P

HEAD_SIZE = 128


def in_blocks(value, dim, length):
    before, after = (value.shape[:dim], value.shape[dim + 1 :])
    return jnp.moveaxis(value.reshape(*before, length, -1, *after), dim, 0)


def sum_at_owner(value, axis, dim):
    length = lax.axis_size(axis)
    blocks = lax.all_to_all(in_blocks(value, dim, length), axis, 0, 0, tiled=True)
    return jnp.sum(blocks, axis=0)


def on_device(
    queries,
    keys,
    values,
    document_index,
    out_proj,
    residual_in,
    norm_gain,
    expert_ids,
    gate_weights,
    w_gate_up,
    w_down,
):
    token_group = queries.shape[0]
    kv_dev = keys.shape[1] // HEAD_SIZE
    query_dev = queries.shape[1] // HEAD_SIZE
    group_ratio = query_dev // kv_dev
    model_width = residual_in.shape[1]
    query_head_split = queries.reshape(token_group, kv_dev, group_ratio, HEAD_SIZE)
    key_head_split = keys.reshape(token_group, kv_dev, HEAD_SIZE)
    value_head_split = values.reshape(token_group, kv_dev, HEAD_SIZE)
    scores = jnp.einsum(
        "qgrd,kgd->grqk", query_head_split, key_head_split, preferred_element_type=jnp.float32
    ) * (1.0 / HEAD_SIZE**0.5)
    doc_row = document_index[0]
    positions = jnp.arange(token_group, dtype=jnp.int32)
    visible = (positions[:, None] >= positions[None, :]) & (doc_row[:, None] == doc_row[None, :])
    scores = jnp.where(visible, scores, -jnp.inf)
    row_max = jnp.max(scores, axis=-1, keepdims=True)
    exponent = jnp.where(visible, jnp.exp(scores - row_max), 0.0)
    weights = (exponent / jnp.sum(exponent, axis=-1, keepdims=True)).astype(jnp.bfloat16)
    head_out = jnp.einsum(
        "grqk,kgd->qgrd", weights, value_head_split, preferred_element_type=jnp.float32
    )
    head_out = head_out.astype(jnp.bfloat16).reshape(token_group, query_dev * HEAD_SIZE)
    partial_value = jnp.dot(
        head_out,
        lax.all_gather(out_proj, "group", axis=1, tiled=True),
        preferred_element_type=jnp.float32,
    )
    attended = sum_at_owner(partial_value, "tensor", 0)
    hidden = residual_in.astype(jnp.float32) + attended
    mean_square = jnp.mean(hidden * hidden, axis=-1, keepdims=True)
    normed = (hidden * lax.rsqrt(mean_square + 1e-06) * norm_gain).astype(jnp.bfloat16)
    tok_dev, top_count = expert_ids.shape
    experts = lax.axis_size("group") * lax.axis_size("tensor")
    capacity = 2 * tok_dev * top_count // experts
    flat_ids = expert_ids.reshape(-1)
    matches = (flat_ids[:, None] == jnp.arange(experts, dtype=jnp.int32)[None, :]).astype(jnp.int32)
    before = jnp.cumsum(matches, axis=0) - matches
    position = jnp.sum(before * matches, axis=1)
    slot_index = flat_ids * capacity + position
    slot_rows = jnp.arange(experts * capacity, dtype=jnp.int32)
    routing_table = jnp.any(
        slot_rows[:, None, None] == slot_index.reshape(1, tok_dev, top_count), axis=-1
    )
    outgoing = jnp.dot(
        routing_table.astype(jnp.bfloat16), normed, preferred_element_type=jnp.float32
    )
    outgoing = outgoing.astype(jnp.bfloat16).reshape(experts, capacity, model_width)
    gate_up = w_gate_up[0]
    down_rows = w_down[0]
    ff_width = down_rows.shape[0]
    block = lax.all_to_all(outgoing, ("group", "tensor"), split_axis=0, concat_axis=0, tiled=True)
    flat_rows = block.reshape(-1, model_width)
    projected = jnp.dot(flat_rows, gate_up, preferred_element_type=jnp.float32)
    activated = (jax.nn.silu(projected[:, :ff_width]) * projected[:, ff_width:]).astype(
        jnp.bfloat16
    )
    expert_out = jnp.dot(activated, down_rows, preferred_element_type=jnp.float32).astype(
        jnp.bfloat16
    )
    results = lax.all_to_all(
        expert_out.reshape(block.shape),
        ("group", "tensor"),
        split_axis=0,
        concat_axis=0,
        tiled=True,
    )
    results = results.reshape(experts * capacity, model_width)
    picked = results[slot_index].astype(jnp.float32).reshape(tok_dev, top_count, model_width)
    expert_sum = jnp.sum(picked * gate_weights[:, :, None], axis=1)
    return (hidden + expert_sum).astype(jnp.bfloat16)


def solution(mesh):
    in_specs = (
        P("group", "tensor"),
        P("group", "tensor"),
        P("group", "tensor"),
        P("group", None),
        P("tensor", "group"),
        P(("group", "tensor"), None),
        P(),
        P(("group", "tensor"), None),
        P(("group", "tensor"), None),
        P(("group", "tensor"), None, None),
        P(("group", "tensor"), None, None),
    )
    out_specs = P(("group", "tensor"), None)
    return jax.shard_map(
        on_device, mesh=mesh, in_specs=in_specs, out_specs=out_specs, check_vma=False
    )
```

profile of v0, /device:TPU:1, one launch (start us, length us, event | category | flops | bytes accessed | tf_op | source)
XLA Modules:
  0.0 290.3 jit_solution(9968445289214750433)
XLA Ops:
  6.5 0.7 all-gather.2.cloned.1.call-update
  7.3 0.8 fusion.29
  8.1 1.0 fusion.35
  9.1 0.1 fusion.17
  9.2 1.0 fusion.13
  10.3 0.2 copy.27
  10.4 0.1 dot_general.22
  10.6 61.5 %all-gather.2.cloned.1.call-done = bf16[1024,4096]{1,0:T(8,128)(2,1)} async-done(((bf16[1024,128]{1,0:T(8,128)(2,1)}), bf16[1024,4096]{1,0:T(8,128)(2,1)}) %all-gather.2.cloned.1.call-update) | async-done | bytes 8388624 | tf_op jit(solution)/shard_map/all_gather | solution.py:57
  72.1 6.0 %fusion.2 = f32[4,32,4096]{2,1,0:T(8,128)} fusion(bf16[4,32,1024]{2,1,0:T(8,128)(2,1)S(1)} %dot_general.22, bf16[1024,4096]{1,0:T(8,128)(2,1)} %all-gather.2.cloned.1.call-done), kind=kOutput, calls=%fused_computation.3 | convolution fusion | flops 1073741824 | bytes 10747904 | tf_op jit(solution)/shard_map/dot_general | solution.py:55
  78.1 4.1 %all-to-all-start = ((f32[4,32,4096]{2,1,0:T(8,128)}), f32[4,32,4096]{2,1,0:T(8,128)S(1)}, u32[]{:S(2)}, u32[]{:S(2)}) async-start(f32[4,32,4096]{2,1,0:T(8,128)} %fusion.2), calls=%async_computation | async-start | bytes 4194304 | tf_op jit(solution)/shard_map/all_to_all | solution.py:16
  82.3 0.1 eq.62
  82.4 0.1 eq.58
  82.5 0.1 copy.31
  82.6 0.2 fusion.24
  82.9 0.2 fusion.26
  83.2 0.2 fusion.16
  83.5 24.7 %all-to-all-done = f32[4,32,4096]{2,1,0:T(8,128)S(1)} async-done(((f32[4,32,4096]{2,1,0:T(8,128)}), f32[4,32,4096]{2,1,0:T(8,128)S(1)}, u32[]{:S(2)}, u32[]{:S(2)}) %all-to-all-start) | async-done | bytes 2097184 | tf_op jit(solution)/shard_map/all_to_all | solution.py:16
  108.1 0.1 reduce_sum.50
  108.3 0.2 multiply_reduce_fusion
  108.5 3.3 %convolution_convert_fusion = bf16[512,4096]{1,0:T(8,128)(2,1)} fusion(pred[512,32]{0,1:T(8,128)(4,1)S(1)} %fusion.16, f32[4096]{0:T(1024)S(1)} %copy-done.3, f32[32]{0:T(128)S(1)} %add_rsqrt_fusion, f32[32,4096]{1,0:T(8,128)S(1)} %reduce_sum.50, bf16[32,4096]{1,0:T(8,128)(2,1)S(1)} %copy-done.2), kind=kOutput, calls=%fused_computation.8 | convolution fusion | flops 136970240 | bytes 5013632 | tf_op jit(solution)/shard_map/dot_general | solution.py:76
  111.8 7.2 %reshape.116 = bf16[128,4,4096]{2,1,0:T(4,128)(2,1)} reshape(bf16[512,4096]{1,0:T(8,128)(2,1)} %convolution_convert_fusion) | data formatting | bytes 8388608 | tf_op jit(solution)/shard_map/reshape | solution.py:79
  119.0 60.3 %all_to_all.15 = bf16[128,4,4096]{2,1,0:T(4,128)(2,1)} all-to-all(bf16[128,4,4096]{2,1,0:T(4,128)(2,1)} %reshape.116), channel_id=1, replica_groups=mesh['group'=32,'tensor'=4] {'group','tensor'}, dimensions={0} | all-to-all | bytes 8388608 | tf_op jit(solution)/shard_map/all_to_all | solution.py:83
  179.3 7.1 %reshape.117 = bf16[512,4096]{1,0:T(8,128)(2,1)} reshape(bf16[128,4,4096]{2,1,0:T(4,128)(2,1)} %all_to_all.15) | data formatting | bytes 8388608 | tf_op jit(solution)/shard_map/reshape | solution.py:84
  186.4 10.6 %fusion = f32[512,1536]{1,0:T(8,128)S(1)} fusion(bf16[512,4096]{1,0:T(8,128)(2,1)} %reshape.117, bf16[1,4096,1536]{2,1,0:T(8,128)(2,1)} %param.20), kind=kOutput, calls=%fused_computation.1 | convolution fusion | flops 6442450944 | bytes 19922944 | tf_op jit(solution)/shard_map/dot_general | solution.py:85
  197.1 5.1 %fusion.6 = bf16[512,4096]{1,0:T(8,128)(2,1)} fusion(bf16[1,768,4096]{2,1,0:T(8,128)(2,1)S(1)} %bitcast.76, f32[512,1536]{1,0:T(8,128)S(1)} %fusion), kind=kOutput, calls=%fused_computation.7 | convolution fusion | flops 3225681920 | bytes 13631488 | tf_op jit(solution)/shard_map/dot_general | solution.py:89
  202.2 7.2 %reshape.118 = bf16[128,4,4096]{2,1,0:T(4,128)(2,1)} reshape(bf16[512,4096]{1,0:T(8,128)(2,1)} %fusion.6) | data formatting | bytes 8388608 | tf_op jit(solution)/shard_map/reshape | solution.py:93
  209.4 5.1 %all-to-all-start.2 = ((bf16[128,4,4096]{2,1,0:T(4,128)(2,1)}), bf16[128,4,4096]{2,1,0:T(4,128)(2,1)}, u32[]{:S(2)}, u32[]{:S(2)}) async-start(bf16[128,4,4096]{2,1,0:T(4,128)(2,1)} %reshape.118), calls=%async_computation.2 | async-start | bytes 8388608 | tf_op jit(solution)/shard_map/all_to_all | solution.py:92
  214.6 52.8 %all-to-all-done.2 = bf16[128,4,4096]{2,1,0:T(4,128)(2,1)} async-done(((bf16[128,4,4096]{2,1,0:T(4,128)(2,1)}), bf16[128,4,4096]{2,1,0:T(4,128)(2,1)}, u32[]{:S(2)}, u32[]{:S(2)}) %all-to-all-start.2) | async-done | bytes 4194336 | tf_op jit(solution)/shard_map/all_to_all | solution.py:92
  267.4 6.9 %reshape.119 = bf16[512,4096]{1,0:T(8,128)(2,1)} reshape(bf16[128,4,4096]{2,1,0:T(4,128)(2,1)} %all-to-all-done.2) | data formatting | bytes 8388608 | tf_op jit(solution)/shard_map/reshape | solution.py:99
  274.3 6.7 %gather_fusion = bf16[256,4096]{1,0:T(8,128)(2,1)S(1)} fusion(bf16[512,4096]{1,0:T(8,128)(2,1)} %reshape.119, s32[1024]{0:T(1024)S(1)} %pad_clamp_fusion), kind=kCustom, calls=%fused_computation | custom fusion | bytes 4195328 | tf_op jit(solution)/shard_map/gather | solution.py:100
  281.0 1.6 fusion.9
  282.6 0.8 add_convert_fusion
  (32 shorter events, 0.5 us)
Async XLA Ops:
  6.5 1.5 copy-start
  6.5 65.5 %all-gather.2.cloned.1.call-start = ((), (), s32[]{:S(2)}) async-start(), calls=%async_computation.3 | async-start | bytes 8650752 | tf_op jit(solution)/shard_map/all_gather | solution.py:57
  78.1 4.1 %copy-start.4 = (s32[32,8]{0,1:T(8,128)S(1)}, s32[32,8]{0,1:T(8,128)}, u32[]{:S(2)}) copy-start(s32[32,8]{0,1:T(8,128)} %param.18) | copy-start | bytes 3076
  78.1 30.2 %copy-start.2 = (bf16[32,4096]{1,0:T(8,128)(2,1)S(1)}, bf16[32,4096]{1,0:T(8,128)(2,1)}, u32[]{:S(2)}) copy-start(bf16[32,4096]{1,0:T(8,128)(2,1)} %param.16) | copy-start | bytes 786436
  78.1 30.4 %copy-start.3 = (f32[4096]{0:T(1024)S(1)}, f32[4096]{0:T(1024)}, u32[]{:S(2)}) copy-start(f32[4096]{0:T(1024)} %param.17) | copy-start | bytes 49156
  78.1 30.0 %all-to-all-start = ((f32[4,32,4096]{2,1,0:T(8,128)}), f32[4,32,4096]{2,1,0:T(8,128)S(1)}, u32[]{:S(2)}, u32[]{:S(2)}) async-start(f32[4,32,4096]{2,1,0:T(8,128)} %fusion.2), calls=%async_computation | async-start | bytes 4194304 | tf_op jit(solution)/shard_map/all_to_all | solution.py:16
  179.3 17.7 %slice-start = ((s8[6291456]{0:T(1024)(128)(4,1)}), s8[2097152]{0:T(1024)(128)(4,1)S(1)}, s32[]{:S(2)}) async-start(s8[6291456]{0:T(1024)(128)(4,1)} %bitcast.75), calls=%async_computation.4 | async-start | bytes 4194304
  186.4 10.7 %slice-start.1 = ((s8[6291456]{0:T(1024)(128)(4,1)}), s8[4194304]{0:T(1024)(128)(4,1)S(1)}, s32[]{:S(2)}) async-start(s8[6291456]{0:T(1024)(128)(4,1)} %bitcast.75), calls=%async_computation.5 | async-start | bytes 8388608
  209.4 5.2 %copy-start.5 = (f32[32,8]{0,1:T(8,128)S(1)}, f32[32,8]{0,1:T(8,128)}, u32[]{:S(2)}) copy-start(f32[32,8]{0,1:T(8,128)} %param.19) | copy-start | bytes 3076
  209.4 58.1 %all-to-all-start.2 = ((bf16[128,4,4096]{2,1,0:T(4,128)(2,1)}), bf16[128,4,4096]{2,1,0:T(4,128)(2,1)}, u32[]{:S(2)}, u32[]{:S(2)}) async-start(bf16[128,4,4096]{2,1,0:T(4,128)(2,1)} %reshape.118), calls=%async_computation.2 | async-start | bytes 8388608 | tf_op jit(solution)/shard_map/all_to_all | solution.py:92
  274.3 9.1 %copy-start.1 = (bf16[128,1024]{1,0:T(8,128)(2,1)S(1)}, bf16[128,1024]{1,0:T(8,128)(2,1)}, u32[]{:S(2)}) copy-start(bf16[128,1024]{1,0:T(8,128)(2,1)} %param.11) | copy-start | bytes 786436
Sparse Core Ops, SparseCore 0:
  9.5 62.5 all-gather.1
where the time goes:
time: 291 us; the launch traced here: 290 us
  waiting for transfers between devices  140 us (48%)
  blocking collectives  60.3 us (21%)
  local copies, waits for them, and re-layouts  36 us (12%)
  matrix products  27.1 us (9%)
  between operations  13.6 us (5%)
  starting transfers between devices  9.2 us (3%)
  other arithmetic  4.38 us (2%)
    all_gather x1, waiting for transfers between devices, on_device(): lax.all_gather(out_proj, 'group', axis=1, tiled=True)  61.5 us
    all_to_all x1, blocking collectives, on_device(): lax.all_to_all(outgoing, ('group', 'tensor'), split_axis=0, concat_axis=0...  60.3 us
    all_to_all x1, waiting for transfers between devices, on_device(): lax.all_to_all(expert_out.reshape(block.shape), ('group', 'tensor'), spli...  52.8 us
    all_to_all x1, waiting for transfers between devices, sum_at_owner(): lax.all_to_all(in_blocks(value, dim, length), axis, 0, 0, tiled=True)  24.7 us
    dot_general x1, matrix products, on_device(): projected = jnp.dot(flat_rows, gate_up, preferred_element_type=jnp.float32)  10.6 us
    reshape x1, local copies, waits for them, and re-layouts, on_device(): outgoing.astype(jnp.bfloat16).reshape(experts, capacity, model_width)  7.2 us
    reshape x1, local copies, waits for them, and re-layouts, on_device(): expert_out.reshape(block.shape)  7.19 us
    reshape x1, local copies, waits for them, and re-layouts, on_device(): flat_rows = block.reshape(-1, model_width)  7.07 us
  transfers between devices with their start and end apart: 3, of which 3 were waited for; matrix products, arithmetic and copies ran while one was open for 2% of the time, Pallas kernels for 0%

commit v1 on v0

v1 whole, which is shorter than its diff:
```python
import functools

import jax
import jax.numpy as jnp
from jax import lax
from jax.experimental import pallas as pl
from jax.experimental.pallas import tpu as pltpu
from jax.sharding import PartitionSpec as P

HEAD = 128
MODEL = 4096
FF = 768
TOK = 32
CHUNKS = (
    (0, 0, 768, 0),
    (1, 1408, 640, 0),
    (2, 2688, 640, 0),
    (0, 768, 640, 1),
    (1, 2048, 640, 1),
    (2, 3328, 768, 1),
)
BF = jnp.bfloat16
F32 = jnp.float32


def dot(a, b):
    return jnp.dot(a, b, preferred_element_type=F32)


def device(x, y, z, c):
    return {"group": (x * 4 + z) * 2 + c, "tensor": y}


def plane_index(a, x, y, z, c):
    if a == 0:
        return c * 16 + z * 4 + y
    if a == 1:
        return c * 16 + z * 4 + x
    return c * 16 + x * 4 + y


def plane_partner(a, x, y, z, c, k):
    nc = lax.rem(c + lax.rem(k, 2), 2)
    lo = lax.rem(k // 2, 4)
    hi = k // 8
    if a == 0:
        return x, lax.rem(y + lo, 4), lax.rem(z + hi, 4), nc
    if a == 1:
        return lax.rem(x + lo, 4), y, lax.rem(z + hi, 4), nc
    return lax.rem(x + hi, 4), lax.rem(y + lo, 4), z, nc


def line_partner(a, x, y, z, d):
    if a == 0:
        return lax.rem(x + d, 4), y, z
    if a == 1:
        return x, lax.rem(y + d, 4), z
    return x, y, lax.rem(z + d, 4)


def axis_row(a, canon):
    r = canon & 3
    y = (canon >> 2) & 3
    x = (canon >> 4) & 3
    z = (canon >> 6) & 3
    if a == 0:
        return z * 64 + y * 16 + x * 4 + r
    return x * 64 + y * 16 + z * 4 + r


def iota(shape, dim):
    return lax.broadcasted_iota(jnp.int32, shape, dim)


def kernel(
    q_ref, k_ref, v_ref, doc_ref, wo_ref, res_ref, gain_ref, meta_ref, w1_hbm, w2_hbm, out_ref, *scratch
):
    n = len(CHUNKS)
    (w1, w2, b_buf, a_buf, c_send, c_recv, hid, proj, act, act_p, meta_all, sel, wgt_hi, wgt_lo, perm, perm_t) = scratch[:16]
    rest = scratch[16:]
    gath, slot_send, slot_recv, ret_recv, part, part_recv = (rest[i * n : (i + 1) * n] for i in range(6))
    (
        w_sem, b_send_sem, b_recv_sem, b_sib_sem, a_send_sem, a_recv_sem, c_send_sem, c_recv_sem, m_send_sem, m_recv_sem,
        g_send_sem, g_recv_sem, s_send_sem, s_recv_sem, y_send_sem, y_recv_sem, z_send_sem, z_recv_sem,
    ) = rest[6 * n :]

    g = lax.axis_index("group")
    y = lax.axis_index("tensor")
    x = g // 8
    z = lax.rem(g // 2, 4)
    c = lax.rem(g, 2)
    me = (x, y, z, c)
    along = (x, y, z)

    def remote(src, dst, send, recv, to):
        return pltpu.make_async_remote_copy(
            src_ref=src, dst_ref=dst, send_sem=send, recv_sem=recv, device_id=device(*to)
        )

    def wait_bytes(ref, sem):
        pltpu.make_async_copy(ref, ref, sem).wait()

    barrier = pltpu.get_barrier_semaphore()

    def greet(i, _):
        pl.semaphore_signal(
            barrier,
            inc=1,
            device_id={"group": lax.rem(g + i // 4, 32), "tensor": lax.rem(y + lax.rem(i, 4), 4)},
        )
        return 0

    lax.fori_loop(1, 128, greet, 0)

    loads = []
    for i in range(4):
        loads.append(
            pltpu.make_async_copy(w1_hbm.at[0, pl.ds(i * 1024, 1024)], w1.at[pl.ds(i * 1024, 1024)], w_sem.at[i])
        )
    for i in range(2):
        loads.append(
            pltpu.make_async_copy(w2_hbm.at[0, pl.ds(i * 384, 384)], w2.at[pl.ds(i * 384, 384)], w_sem.at[4 + i])
        )
    for copy in loads:
        copy.start()

    doc = jnp.broadcast_to(doc_ref[...].astype(F32), (128, 128))
    visible = (doc == doc.T) & (iota((128, 128), 0) >= iota((128, 128), 1))
    keys = k_ref[...]
    vals = v_ref[...]

    def attend(h):
        query = q_ref[:, h * HEAD : (h + 1) * HEAD]
        scores = lax.dot_general(query, keys, (((1,), (1,)), ((), ())), preferred_element_type=F32)
        scores = jnp.where(visible, scores * (1.0 / HEAD**0.5), -1e30)
        top = jnp.max(scores, axis=-1, keepdims=True)
        expo = jnp.where(visible, jnp.exp(scores - top), 0.0)
        weights = (expo / jnp.sum(expo, axis=-1, keepdims=True)).astype(BF)
        a_buf[z, :, h * HEAD : (h + 1) * HEAD] = dot(weights, vals).astype(BF)

    def send_heads(half):
        cols = pl.ds(half * 512, 512)
        for d in (1, 3, 2):
            to = (x, y, lax.rem(z + d, 4), c)
            remote(a_buf.at[z, :, cols], a_buf.at[z, :, cols], a_send_sem, a_recv_sem.at[d - 1], to).start()

    def b_cols(xx, cc):
        return pl.ds(pl.multiple_of((xx * 2 + cc) * 128, 128), 128)

    for h in range(4):
        attend(h)
    pl.semaphore_wait(barrier, 127)
    sibling = (x, y, z, 1 - c)
    for d in (2, 1, 3):
        to = (lax.rem(x + d, 4), y, z, c)
        remote(wo_ref, b_buf.at[:, b_cols(x, c)], b_send_sem, b_recv_sem.at[d - 1], to).start()
    remote(wo_ref, b_buf.at[:, b_cols(x, c)], b_send_sem, b_sib_sem, sibling).start()
    send_heads(0)
    for a in range(3):
        for d in (1, 3, 2):
            to = line_partner(a, x, y, z, d) + (c,)
            remote(meta_ref, meta_all.at[a, along[a]], m_send_sem, m_recv_sem, to).start()
    for h in range(4, 8):
        attend(h)
    send_heads(1)
    b_buf[:, b_cols(x, c)] = wo_ref[...]

    for a in range(3):
        meta_all[a, along[a]] = meta_ref[...]
    canon = iota((256, 256), 0)
    canon_t = iota((256, 256), 1)
    for i, a in enumerate((0, 2)):
        perm[i] = (iota((256, 256), 1) == axis_row(a, canon)).astype(F32).astype(BF)
        perm_t[i] = (iota((256, 256), 0) == axis_row(a, canon_t)).astype(F32).astype(BF)
    wait_bytes(meta_all9(meta_all), m_recv_sem)
    lane = iota((128, 128), 1)
    row = iota((128, 128), 0)
    earlier = (((row >> 5) == (lane >> 5)) & (row < lane)).astype(F32).astype(BF)
    slot = iota((512, 128), 0)
    slot_lane = iota((512, 128), 1)
    for a in range(3):
        meta = jnp.zeros((16, 128), F32)
        for s in range(4):
            meta = jnp.where((iota((16, 128), 1) >> 5) == s, meta_all[a, s], meta)
        named = jnp.zeros((128, 128), F32)
        gate = jnp.zeros((128, 128), F32)
        row_f = row.astype(F32)
        for k in range(8):
            hit = jnp.broadcast_to(meta[k : k + 1], (128, 128)) == row_f
            named = jnp.where(hit, 1.0, named)
            gate = jnp.where(hit, jnp.broadcast_to(meta[8 + k : 9 + k], (128, 128)), gate)
        place = dot(named.astype(BF), earlier)
        place = jnp.where(named > 0.5, place + 1.0, 0.0).astype(BF)
        gate_hi = gate.astype(BF)
        gate_lo = (gate - gate_hi.astype(F32)).astype(BF)
        j = slot >> 4
        jc, jh, jl = j >> 4, (j >> 2) & 3, j & 3
        if a == 0:
            ex, ey, ez = x, jl, jh
        elif a == 1:
            ex, ey, ez = jl, y, jh
        else:
            ex, ey, ez = jh, jl, z
        expert = ((ex * 4 + ez) * 2 + jc) * 4 + ey
        pick = (slot_lane == expert).astype(F32).astype(BF)
        match = (dot(pick, place) == ((slot & 3) + 1).astype(F32)) & ((slot_lane >> 5) == ((slot >> 2) & 3))
        sel[a] = jnp.where(match, 1.0, 0.0).astype(BF)
        wgt_hi[a] = jnp.where(match, dot(pick, gate_hi), 0.0).T.astype(BF)
        wgt_lo[a] = jnp.where(match, dot(pick, gate_lo), 0.0).T.astype(BF)

    for d in (1, 3, 2):
        src = lax.rem(x + 4 - d, 4)
        block = b_buf.at[:, b_cols(src, c)]
        wait_bytes(block, b_recv_sem.at[d - 1])
        remote(block, block, b_send_sem, b_sib_sem, sibling).start()
    wait_bytes(b_buf.at[:, pl.ds(0, 512)], b_sib_sem)
    for d in (0, 1, 3, 2):
        zz = lax.rem(z + 4 - d, 4)
        if d:
            wait_bytes(a_buf.at[zz], a_recv_sem.at[d - 1])

        def project(t, _, zz=zz):
            cols = pl.ds(pl.multiple_of(t * 256, 256), 256)
            c_send[zz, :, cols] = dot(a_buf[zz], b_buf[:, cols]).astype(BF)
            return 0

        lax.fori_loop(0, 4, project, 0)
        for dy in (1, 3, 2, 0):
            yy = lax.rem(y + dy, 4)
            rows = pl.ds(pl.multiple_of(yy * TOK, TOK), TOK)
            if d or dy:
                remote(
                    c_send.at[zz, rows, :], c_recv.at[y * 4 + z], c_send_sem, c_recv_sem, (x, yy, zz, c)
                ).start()
            else:
                c_recv[y * 4 + z] = c_send[zz, rows, :]
    wait_bytes(c_recv.at[pl.ds(0, 15)], c_recv_sem)
    square = jnp.zeros((TOK, 256), F32)
    for zz in range(4):
        for xx in range(4):
            col = (xx * 4 + zz) * 256
            value = res_ref[:, col : col + 256].astype(F32)
            for yy in range(4):
                value = value + c_recv[yy * 4 + zz, :, xx * 256 : (xx + 1) * 256].astype(F32)
            hid[:, col : col + 256] = value
            square = square + value * value
    scale = lax.rsqrt(jnp.sum(square, axis=-1, keepdims=True) * (1.0 / MODEL) + 1e-06)

    for i, (a, col, width, _) in enumerate(CHUNKS):
        normed = (hid[:, col : col + width] * scale * gain_ref[:, col : col + width]).astype(BF)
        gath[i][along[a]] = normed
        for d in (1, 3, 2):
            to = line_partner(a, x, y, z, d) + (c,)
            mine = gath[i].at[along[a]]
            remote(mine, mine, g_send_sem.at[i], g_recv_sem.at[i], to).start()

    def exchange(group, sources, targets, send_sem, recv_sem):
        members = [i for i in range(n) if CHUNKS[i][3] == group]

        def step(k, _):
            for i in members:
                a = CHUNKS[i][0]
                to = plane_partner(a, *me, k)
                remote(
                    sources[i].at[plane_index(a, *to)],
                    targets[i].at[plane_index(a, *me)],
                    send_sem.at[i],
                    recv_sem.at[i],
                    to,
                ).start()
            return 0

        lax.fori_loop(1, 32, step, 0)
        for i in members:
            mine = plane_index(CHUNKS[i][0], *me)
            targets[i][mine] = sources[i][mine]

    for group in range(2):
        for i, (a, col, width, grp) in enumerate(CHUNKS):
            if grp == group:
                wait_bytes(gath[i].at[pl.ds(0, 3)], g_recv_sem.at[i])
                rows = dot(sel[a], gath[i][...].reshape(128, width))
                slot_send[i][...] = rows.astype(BF).reshape(32, 16, width)
        exchange(group, slot_send, slot_recv, s_send_sem, s_recv_sem)

    for copy in loads:
        copy.wait()

    for group in range(2):
        members = [i for i in range(n) if CHUNKS[i][3] == group]
        for i in members:
            a, col, width, _ = CHUNKS[i]
            wait_bytes(slot_recv[i].at[pl.ds(0, 31)], s_recv_sem.at[i])
            if a != 1:
                for half in range(2):
                    block = slot_recv[i][half * 16 : half * 16 + 16].reshape(256, width)
                    moved = dot(perm[a // 2], block).astype(BF)
                    slot_recv[i][half * 16 : half * 16 + 16] = moved.reshape(16, 16, width)

        def up(t, _, members=members, group=group):
            cols = pl.ds(pl.multiple_of(t * 256, 256), 256)
            total = proj[:, cols] if group else jnp.zeros((512, 256), F32)
            for i in members:
                _, col, width, _ = CHUNKS[i]
                total = total + dot(slot_recv[i][...].reshape(512, width), w1[col : col + width, cols])
            proj[:, cols] = total
            return 0

        lax.fori_loop(0, 6, up, 0)

    def activate(t, _):
        rows = pl.ds(pl.multiple_of(t * 64, 64), 64)
        gate = proj[rows, :FF]
        act[rows, :] = (gate / (1.0 + jnp.exp(-gate)) * proj[rows, FF:]).astype(BF)
        return 0

    lax.fori_loop(0, 8, activate, 0)
    for i in range(2):
        for half in range(2):
            rows = slice(half * 256, half * 256 + 256)
            act_p[i, rows, :] = dot(perm_t[i], act[rows, :]).astype(BF)

    for group in range(2):
        for i, (a, col, width, grp) in enumerate(CHUNKS):
            if grp == group:
                wait_bytes(slot_send[i].at[pl.ds(0, 31)], s_send_sem.at[i])
                for t in range(0, width, 128):
                    mine = act[...] if a == 1 else act_p[a // 2]
                    rows = dot(mine, w2[:, col + t : col + t + 128]).astype(BF)
                    slot_send[i][:, :, t : t + 128] = rows.reshape(32, 16, 128)
        exchange(group, slot_send, ret_recv, y_send_sem, y_recv_sem)

    for group in range(2):
        for i, (a, col, width, grp) in enumerate(CHUNKS):
            if grp == group:
                wait_bytes(ret_recv[i].at[pl.ds(0, 31)], y_recv_sem.at[i])
                rows = ret_recv[i][...].reshape(512, width)
                total = dot(wgt_hi[a], rows) + dot(wgt_lo[a], rows)
                part[i][...] = total.astype(BF).reshape(4, TOK, width)
                part_recv[i][along[a]] = part[i][along[a]]
                for d in (1, 3, 2):
                    to = line_partner(a, x, y, z, d) + (c,)
                    remote(
                        part[i].at[lax.rem(along[a] + d, 4)],
                        part_recv[i].at[along[a]],
                        z_send_sem.at[i],
                        z_recv_sem.at[i],
                        to,
                    ).start()
    for i, (a, col, width, _) in enumerate(CHUNKS):
        wait_bytes(part_recv[i].at[pl.ds(0, 3)], z_recv_sem.at[i])
        total = hid[:, col : col + width]
        for s in range(4):
            total = total + part_recv[i][s].astype(F32)
        out_ref[:, col : col + width] = total.astype(BF)

    wait_bytes(b_buf.at[:, pl.ds(0, 896)], b_send_sem)
    wait_bytes(a_buf.at[pl.ds(0, 3)], a_send_sem)
    wait_bytes(c_recv.at[pl.ds(0, 15)], c_send_sem)
    wait_bytes(meta_all9(meta_all), m_send_sem)
    for i in range(n):
        wait_bytes(gath[i].at[pl.ds(0, 3)], g_send_sem.at[i])
        wait_bytes(slot_send[i].at[pl.ds(0, 31)], y_send_sem.at[i])
        wait_bytes(part[i].at[pl.ds(0, 3)], z_send_sem.at[i])


def meta_all9(meta_all):
    return meta_all.at[:, pl.ds(0, 3)]


def on_device(
    queries, keys, values, document_index, out_proj, residual_in, norm_gain, expert_ids, gate_weights, w_gate_up, w_down
):
    meta = jnp.concatenate([expert_ids.astype(F32).T, gate_weights.T], axis=0)
    meta = jnp.tile(meta, (1, 4))
    vmem = pl.BlockSpec(memory_space=pltpu.VMEM)
    hbm = pl.BlockSpec(memory_space=pl.ANY)
    dma = pltpu.SemaphoreType.DMA
    n = len(CHUNKS)

    def buf(*shape, dtype=BF):
        return pltpu.VMEM(shape, dtype)

    widths = [chunk[2] for chunk in CHUNKS]
    scratch = [
        buf(MODEL, 2 * FF),
        buf(FF, MODEL),
        buf(1024, 1024),
        buf(4, 128, 1024),
        buf(4, 128, 1024),
        buf(16, TOK, 1024),
        buf(TOK, MODEL, dtype=F32),
        buf(512, 2 * FF, dtype=F32),
        buf(512, FF),
        buf(2, 512, FF),
        buf(3, 4, 16, 128, dtype=F32),
        buf(3, 512, 128),
        buf(3, 128, 512),
        buf(3, 128, 512),
        buf(2, 256, 256),
        buf(2, 256, 256),
    ]
    scratch += [buf(4, TOK, w) for w in widths]
    for _ in range(3):
        scratch += [buf(32, 16, w) for w in widths]
    for _ in range(2):
        scratch += [buf(4, TOK, w) for w in widths]
    scratch += [
        dma((6,)), dma, dma((3,)), dma, dma, dma((3,)), dma, dma, dma, dma,
        dma((n,)), dma((n,)), dma((n,)), dma((n,)), dma((n,)), dma((n,)), dma((n,)), dma((n,)),
    ]
    return pl.pallas_call(
        kernel,
        out_shape=jax.ShapeDtypeStruct((TOK, MODEL), BF),
        in_specs=[vmem] * 8 + [hbm] * 2,
        out_specs=vmem,
        scratch_shapes=scratch,
        name="layer",
        compiler_params=pltpu.CompilerParams(
            collective_id=0, has_side_effects=True, vmem_limit_bytes=66_000_000
        ),
    )(
        queries, keys, values, document_index, out_proj, residual_in, norm_gain.reshape(1, -1), meta, w_gate_up, w_down
    )


def solution(mesh):
    both = P(("group", "tensor"), None)
    expert = P(("group", "tensor"), None, None)
    pair = P("group", "tensor")
    in_specs = (pair, pair, pair, P("group", None), P("tensor", "group"), both, P(), both, both, expert, expert)
    return jax.shard_map(on_device, mesh=mesh, in_specs=in_specs, out_specs=both, check_vma=False)
```

time: 291 us -> 145 us (0.50)
  Pallas kernels: 0 us -> 141 us
  waiting for transfers between devices: 140 us -> 0 us
  blocking collectives: 60.3 us -> 0 us
  local copies, waits for them, and re-layouts: 36 us -> 2.36 us
  matrix products: 27.1 us -> 0 us
  between operations: 13.6 us -> 0.01 us
  starting transfers between devices: 9.2 us -> 0 us
  other arithmetic: 4.38 us -> 1.38 us
    pallas_call x0 -> x1, Pallas kernels: none -> 141 us  [on_device(): pl.pallas_call(kernel, out_shape=jax.ShapeDtypeStruct((TOK, MODEL), BF),...]
    all_to_all x2 -> x0, waiting for transfers between devices: 77.5 us -> none  [the longest x1 52.8 us: on_device(): lax.all_to_all(expert_out.reshape(block.shape), ('group', 'tensor'), spli...]
    all_gather x1 -> x0, waiting for transfers between devices: 61.5 us -> none  [on_device(): lax.all_gather(out_proj, 'group', axis=1, tiled=True)]
    all_to_all x1 -> x0, blocking collectives: 60.3 us -> none  [on_device(): lax.all_to_all(outgoing, ('group', 'tensor'), split_axis=0, concat_axis=0...]
    reshape x4 -> x0, local copies, waits for them, and re-layouts: 28.4 us -> none  [the longest x1 7.2 us: on_device(): outgoing.astype(jnp.bfloat16).reshape(experts, capacity, model_width)]
    dot_general x6 -> x0, matrix products: 27.1 us -> none  [the longest x1 10.6 us: on_device(): projected = jnp.dot(flat_rows, gate_up, preferred_element_type=jnp.float32)]
    all_to_all x2 -> x0, starting transfers between devices: 9.2 us -> none  [the longest x1 5.06 us: on_device(): lax.all_to_all(expert_out.reshape(block.shape), ('group', 'tensor'), spli...]
    gather x1 -> x0, local copies, waits for them, and re-layouts: 6.65 us -> none  [on_device(): results[slot_index].astype(jnp.float32)]
  transfers between devices with their start and end apart: 3 -> 0, of which waited for: 3 -> 0; matrix products, arithmetic and copies ran while one was open for 2% -> 0% of each run, Pallas kernels for 0% -> 0%
where the time goes in v1:
time: 145 us
  Pallas kernels  141 us (97%)
  local copies, waits for them, and re-layouts  2.36 us (2%)
    pallas_call x1, Pallas kernels, on_device(): pl.pallas_call(kernel, out_shape=jax.ShapeDtypeStruct((TOK, MODEL), BF),...  141 us

profile of v1, /device:TPU:1, one launch (start us, length us, event | category | flops | bytes accessed | tf_op | source)
XLA Modules:
  0.0 145.0 jit_solution(6447858869085693744)
XLA Ops:
  0.0 0.7 convert_bitcast_fusion
  0.7 0.7 pad_maximum_fusion
  1.4 0.7 tile.10.meta_ref
  2.1 141.3 %layer.1 = bf16[32,4096]{1,0:T(8,128)(2,1)} custom-call(bf16[128,1024]{1,0:T(8,128)(2,1)} %q_ref.1, bf16[128,128]{1,0:T(8,128)(2,1)} %k_ref.1, bf16[128,128]{1,0:T(8,128)(2,1)} %v_ref.1, s32[1,128]{1,0:T(1,128)} %doc_ref.1, bf16[1024,128]{1,0:T(8,128)(2,1)} %wo_ref.1, bf16[32,4096]{1,0:T(8,128)(2,1)} %res_ref.1, f32[1,4096]{1,0:T(1,128)} %bitcast.4, ...), custom_call_target="tpu_custom_call" | custom-call | tf_op jit(solution)/shard_map/layer/pallas_call | solution.py:412
  143.4 1.7 %copy.13 = bf16[32,4096]{1,0:T(8,128)(2,1)} copy(bf16[32,4096]{1,0:T(8,128)(2,1)} %layer.1) | data formatting | bytes 524288
  (1 shorter events, 0.0 us)

commit v2 on v1

--- a/solution.py
+++ b/solution.py
@@ -12,13 +12,17 @@
 FF = 768
 TOK = 32
 CHUNKS = (
-    (0, 0, 768, 0),
-    (1, 1408, 640, 0),
-    (2, 2688, 640, 0),
-    (0, 768, 640, 1),
-    (1, 2048, 640, 1),
-    (2, 3328, 768, 1),
+    (1, 1280, 512, 0),
+    (0, 0, 512, 0),
+    (2, 2560, 512, 0),
+    (1, 1792, 512, 1),
+    (0, 512, 512, 1),
+    (2, 3072, 512, 1),
+    (1, 2304, 256, 2),
+    (0, 1024, 256, 2),
+    (2, 3584, 512, 2),
 )
+GROUPS = 3
 BF = jnp.bfloat16
 F32 = jnp.float32
 
@@ -73,11 +77,11 @@
 
 
 def kernel(
-    q_ref, k_ref, v_ref, doc_ref, wo_ref, res_ref, gain_ref, meta_ref, w1_hbm, w2_hbm, out_ref, *scratch
+    q_ref, k_ref, v_ref, doc_ref, wo_ref, res_ref, gain_ref, ids_ref, gates_ref, w1_hbm, w2_hbm, out_ref, *scratch
 ):
     n = len(CHUNKS)
-    (w1, w2, b_buf, a_buf, c_send, c_recv, hid, proj, act, act_p, meta_all, sel, wgt_hi, wgt_lo, perm, perm_t) = scratch[:16]
-    rest = scratch[16:]
+    (w1, w2, b_buf, a_buf, c_send, c_recv, hid, proj, act, act_p, meta, turn, meta_all, sel, wgt, perm, perm_t) = scratch[:17]
+    rest = scratch[17:]
     gath, slot_send, slot_recv, ret_recv, part, part_recv = (rest[i * n : (i + 1) * n] for i in range(6))
     (
         w_sem, b_send_sem, b_recv_sem, b_sib_sem, a_send_sem, a_recv_sem, c_send_sem, c_recv_sem, m_send_sem, m_recv_sem,
@@ -102,15 +106,16 @@
 
     barrier = pltpu.get_barrier_semaphore()
 
-    def greet(i, _):
-        pl.semaphore_signal(
-            barrier,
-            inc=1,
-            device_id={"group": lax.rem(g + i // 4, 32), "tensor": lax.rem(y + lax.rem(i, 4), 4)},
-        )
+    def greet(to):
+        pl.semaphore_signal(barrier, inc=1, device_id=device(*to))
         return 0
 
-    lax.fori_loop(1, 128, greet, 0)
+    def moved(dx, dy, dz, dc):
+        return lax.rem(x + dx, 4), lax.rem(y + dy, 4), lax.rem(z + dz, 4), lax.rem(c + dc, 2)
+
+    lax.fori_loop(1, 32, lambda k, _: greet(moved(k // 8, 0, lax.rem(k // 2, 4), lax.rem(k, 2))), 0)
+    lax.fori_loop(8, 32, lambda k, _: greet(moved(0, k // 8, lax.rem(k // 2, 4), lax.rem(k, 2))), 0)
+    lax.fori_loop(6, 24, lambda k, _: greet(moved(k // 6, 1 + lax.rem(k // 2, 3), 0, lax.rem(k, 2))), 0)
 
     loads = []
     for i in range(4):
@@ -147,26 +152,34 @@
     def b_cols(xx, cc):
         return pl.ds(pl.multiple_of((xx * 2 + cc) * 128, 128), 128)
 
+    for s in range(4):
+        turn[s * TOK : (s + 1) * TOK, 0:8] = ids_ref[...].astype(F32)
+    meta[0:8] = turn[...].T[0:8]
+    for s in range(4):
+        turn[s * TOK : (s + 1) * TOK, 0:8] = gates_ref[...]
+    meta[8:16] = turn[...].T[0:8]
     for h in range(4):
         attend(h)
-    pl.semaphore_wait(barrier, 127)
+    pl.semaphore_wait(barrier, 73)
     sibling = (x, y, z, 1 - c)
-    for d in (2, 1, 3):
+    remote(wo_ref, b_buf.at[:, b_cols(x, c)], b_send_sem, b_sib_sem.at[0], sibling).start()
+    for d in (1, 3):
         to = (lax.rem(x + d, 4), y, z, c)
         remote(wo_ref, b_buf.at[:, b_cols(x, c)], b_send_sem, b_recv_sem.at[d - 1], to).start()
-    remote(wo_ref, b_buf.at[:, b_cols(x, c)], b_send_sem, b_sib_sem, sibling).start()
-    send_heads(0)
     for a in range(3):
         for d in (1, 3, 2):
             to = line_partner(a, x, y, z, d) + (c,)
-            remote(meta_ref, meta_all.at[a, along[a]], m_send_sem, m_recv_sem, to).start()
+            remote(meta, meta_all.at[a, along[a]], m_send_sem, m_recv_sem, to).start()
+    to = (lax.rem(x + 2, 4), y, z, c)
+    remote(wo_ref, b_buf.at[:, b_cols(x, c)], b_send_sem, b_recv_sem.at[1], to).start()
+    send_heads(0)
     for h in range(4, 8):
         attend(h)
     send_heads(1)
     b_buf[:, b_cols(x, c)] = wo_ref[...]
 
     for a in range(3):
-        meta_all[a, along[a]] = meta_ref[...]
+        meta_all[a, along[a]] = meta[...]
     canon = iota((256, 256), 0)
     canon_t = iota((256, 256), 1)
     for i, a in enumerate((0, 2)):
@@ -179,16 +192,16 @@
     slot = iota((512, 128), 0)
     slot_lane = iota((512, 128), 1)
     for a in range(3):
-        meta = jnp.zeros((16, 128), F32)
+        info = jnp.zeros((16, 128), F32)
         for s in range(4):
-            meta = jnp.where((iota((16, 128), 1) >> 5) == s, meta_all[a, s], meta)
+            info = jnp.where((iota((16, 128), 1) >> 5) == s, meta_all[a, s], info)
         named = jnp.zeros((128, 128), F32)
         gate = jnp.zeros((128, 128), F32)
         row_f = row.astype(F32)
         for k in range(8):
-            hit = jnp.broadcast_to(meta[k : k + 1], (128, 128)) == row_f
+            hit = jnp.broadcast_to(info[k : k + 1], (128, 128)) == row_f
             named = jnp.where(hit, 1.0, named)
-            gate = jnp.where(hit, jnp.broadcast_to(meta[8 + k : 9 + k], (128, 128)), gate)
+            gate = jnp.where(hit, jnp.broadcast_to(info[8 + k : 9 + k], (128, 128)), gate)
         place = dot(named.astype(BF), earlier)
         place = jnp.where(named > 0.5, place + 1.0, 0.0).astype(BF)
         gate_hi = gate.astype(BF)
@@ -205,35 +218,59 @@
         pick = (slot_lane == expert).astype(F32).astype(BF)
         match = (dot(pick, place) == ((slot & 3) + 1).astype(F32)) & ((slot_lane >> 5) == ((slot >> 2) & 3))
         sel[a] = jnp.where(match, 1.0, 0.0).astype(BF)
-        wgt_hi[a] = jnp.where(match, dot(pick, gate_hi), 0.0).T.astype(BF)
-        wgt_lo[a] = jnp.where(match, dot(pick, gate_lo), 0.0).T.astype(BF)
-
-    for d in (1, 3, 2):
-        src = lax.rem(x + 4 - d, 4)
-        block = b_buf.at[:, b_cols(src, c)]
-        wait_bytes(block, b_recv_sem.at[d - 1])
-        remote(block, block, b_send_sem, b_sib_sem, sibling).start()
-    wait_bytes(b_buf.at[:, pl.ds(0, 512)], b_sib_sem)
-    for d in (0, 1, 3, 2):
+        wgt[a, 0:128] = jnp.where(match, dot(pick, gate_hi), 0.0).T.astype(BF)
+        wgt[a, 128:256] = jnp.where(match, dot(pick, gate_lo), 0.0).T.astype(BF)
+
+    def project(d, e):
         zz = lax.rem(z + 4 - d, 4)
-        if d:
-            wait_bytes(a_buf.at[zz], a_recv_sem.at[d - 1])
-
-        def project(t, _, zz=zz):
-            cols = pl.ds(pl.multiple_of(t * 256, 256), 256)
-            c_send[zz, :, cols] = dot(a_buf[zz], b_buf[:, cols]).astype(BF)
-            return 0
-
-        lax.fori_loop(0, 4, project, 0)
+        xx = lax.rem(x + 4 - e, 4)
+        cols = pl.ds(pl.multiple_of(xx * 256, 256), 256)
+        c_send[zz, :, cols] = dot(a_buf[zz], b_buf[:, cols]).astype(BF)
         for dy in (1, 3, 2, 0):
             yy = lax.rem(y + dy, 4)
             rows = pl.ds(pl.multiple_of(yy * TOK, TOK), TOK)
             if d or dy:
                 remote(
-                    c_send.at[zz, rows, :], c_recv.at[y * 4 + z], c_send_sem, c_recv_sem, (x, yy, zz, c)
+                    c_send.at[zz, rows, cols], c_recv.at[y * 4 + z, :, cols], c_send_sem, c_recv_sem, (x, yy, zz, c)
                 ).start()
             else:
-                c_recv[y * 4 + z] = c_send[zz, rows, :]
+                c_recv[y * 4 + z, :, cols] = c_send[zz, rows, cols]
+
+    def columns_in(e):
+        xx = lax.rem(x + 4 - e, 4)
+        if e:
+            block = b_buf.at[:, b_cols(xx, c)]
+            wait_bytes(block, b_recv_sem.at[e - 1])
+            remote(block, block, b_send_sem, b_sib_sem.at[e], sibling).start()
+
+    def columns_ready(e):
+        xx = lax.rem(x + 4 - e, 4)
+        wait_bytes(b_buf.at[:, b_cols(xx, 1 - c)], b_sib_sem.at[e])
+
+    def heads_ready(d):
+        wait_bytes(a_buf.at[lax.rem(z + 4 - d, 4)], a_recv_sem.at[d - 1])
+
+    columns_ready(0)
+    project(0, 0)
+    columns_in(1)
+    columns_in(3)
+    columns_ready(1)
+    project(0, 1)
+    columns_ready(3)
+    project(0, 3)
+    heads_ready(1)
+    for e in (0, 1, 3):
+        project(1, e)
+    heads_ready(3)
+    for e in (0, 1, 3):
+        project(3, e)
+    columns_in(2)
+    columns_ready(2)
+    for d in (0, 1, 3):
+        project(d, 2)
+    heads_ready(2)
+    for e in (0, 1, 3, 2):
+        project(2, e)
     wait_bytes(c_recv.at[pl.ds(0, 15)], c_recv_sem)
     square = jnp.zeros((TOK, 256), F32)
     for zz in range(4):
@@ -254,9 +291,7 @@
             mine = gath[i].at[along[a]]
             remote(mine, mine, g_send_sem.at[i], g_recv_sem.at[i], to).start()
 
-    def exchange(group, sources, targets, send_sem, recv_sem):
-        members = [i for i in range(n) if CHUNKS[i][3] == group]
-
+    def exchange(members, sources, targets, send_sem, recv_sem):
         def step(k, _):
             for i in members:
                 a = CHUNKS[i][0]
@@ -275,18 +310,19 @@
             mine = plane_index(CHUNKS[i][0], *me)
             targets[i][mine] = sources[i][mine]
 
-    for group in range(2):
+    for group in range(GROUPS):
         for i, (a, col, width, grp) in enumerate(CHUNKS):
             if grp == group:
                 wait_bytes(gath[i].at[pl.ds(0, 3)], g_recv_sem.at[i])
                 rows = dot(sel[a], gath[i][...].reshape(128, width))
                 slot_send[i][...] = rows.astype(BF).reshape(32, 16, width)
-        exchange(group, slot_send, slot_recv, s_send_sem, s_recv_sem)
+        members = [i for i in range(n) if CHUNKS[i][3] == group]
+        exchange(members, slot_send, slot_recv, s_send_sem, s_recv_sem)
 
     for copy in loads:
         copy.wait()
 
-    for group in range(2):
+    for group in range(GROUPS):
         members = [i for i in range(n) if CHUNKS[i][3] == group]
         for i in members:
             a, col, width, _ = CHUNKS[i]
@@ -320,22 +356,21 @@
             rows = slice(half * 256, half * 256 + 256)
             act_p[i, rows, :] = dot(perm_t[i], act[rows, :]).astype(BF)
 
-    for group in range(2):
-        for i, (a, col, width, grp) in enumerate(CHUNKS):
-            if grp == group:
-                wait_bytes(slot_send[i].at[pl.ds(0, 31)], s_send_sem.at[i])
-                for t in range(0, width, 128):
-                    mine = act[...] if a == 1 else act_p[a // 2]
-                    rows = dot(mine, w2[:, col + t : col + t + 128]).astype(BF)
-                    slot_send[i][:, :, t : t + 128] = rows.reshape(32, 16, 128)
-        exchange(group, slot_send, ret_recv, y_send_sem, y_recv_sem)
-
-    for group in range(2):
+    for i, (a, col, width, _) in enumerate(CHUNKS):
+        wait_bytes(slot_send[i].at[pl.ds(0, 31)], s_send_sem.at[i])
+        for t in range(0, width, 256):
+            mine = act[...] if a == 1 else act_p[a // 2]
+            rows = dot(mine, w2[:, col + t : col + t + 256]).astype(BF)
+            slot_send[i][:, :, t : t + 256] = rows.reshape(32, 16, 256)
+        exchange([i], slot_send, ret_recv, y_send_sem, y_recv_sem)
+
+    for group in range(GROUPS):
         for i, (a, col, width, grp) in enumerate(CHUNKS):
             if grp == group:
                 wait_bytes(ret_recv[i].at[pl.ds(0, 31)], y_recv_sem.at[i])
                 rows = ret_recv[i][...].reshape(512, width)
-                total = dot(wgt_hi[a], rows) + dot(wgt_lo[a], rows)
+                both = dot(wgt[a], rows)
+                total = both[0:128] + both[128:256]
                 part[i][...] = total.astype(BF).reshape(4, TOK, width)
                 part_recv[i][along[a]] = part[i][along[a]]
                 for d in (1, 3, 2):
@@ -371,8 +406,6 @@
 def on_device(
     queries, keys, values, document_index, out_proj, residual_in, norm_gain, expert_ids, gate_weights, w_gate_up, w_down
 ):
-    meta = jnp.concatenate([expert_ids.astype(F32).T, gate_weights.T], axis=0)
-    meta = jnp.tile(meta, (1, 4))
     vmem = pl.BlockSpec(memory_space=pltpu.VMEM)
     hbm = pl.BlockSpec(memory_space=pl.ANY)
     dma = pltpu.SemaphoreType.DMA
@@ -393,10 +426,11 @@
         buf(512, 2 * FF, dtype=F32),
         buf(512, FF),
         buf(2, 512, FF),
+        buf(16, 128, dtype=F32),
+        buf(128, 128, dtype=F32),
         buf(3, 4, 16, 128, dtype=F32),
         buf(3, 512, 128),
-        buf(3, 128, 512),
-        buf(3, 128, 512),
+        buf(3, 256, 512),
         buf(2, 256, 256),
         buf(2, 256, 256),
     ]
@@ -406,13 +440,13 @@
     for _ in range(2):
         scratch += [buf(4, TOK, w) for w in widths]
     scratch += [
-        dma((6,)), dma, dma((3,)), dma, dma, dma((3,)), dma, dma, dma, dma,
+        dma((6,)), dma, dma((3,)), dma((4,)), dma, dma((3,)), dma, dma, dma, dma,
         dma((n,)), dma((n,)), dma((n,)), dma((n,)), dma((n,)), dma((n,)), dma((n,)), dma((n,)),
     ]
     return pl.pallas_call(
         kernel,
         out_shape=jax.ShapeDtypeStruct((TOK, MODEL), BF),
-        in_specs=[vmem] * 8 + [hbm] * 2,
+        in_specs=[vmem] * 9 + [hbm] * 2,
         out_specs=vmem,
         scratch_shapes=scratch,
         name="layer",
@@ -420,7 +454,8 @@
             collective_id=0, has_side_effects=True, vmem_limit_bytes=66_000_000
         ),
     )(
-        queries, keys, values, document_index, out_proj, residual_in, norm_gain.reshape(1, -1), meta, w_gate_up, w_down
+        queries, keys, values, document_index, out_proj, residual_in, norm_gain.reshape(1, -1), expert_ids, gate_weights,
+        w_gate_up, w_down
     )
 
 

time: 145 us -> 130 us (0.90)
  Pallas kernels: 141 us -> 126 us
  local copies, waits for them, and re-layouts: 2.36 us -> 4.39 us
    pallas_call x1, Pallas kernels: 141 us -> 126 us  [on_device(): pl.pallas_call(kernel, out_shape=jax.ShapeDtypeStruct((TOK, MODEL), BF),...]
    unnamed x1 -> x3, local copies, waits for them, and re-layouts: 1.67 us -> 4.39 us
where the time goes in v2:
time: 130 us
  Pallas kernels  126 us (97%)
  local copies, waits for them, and re-layouts  4.39 us (3%)
    pallas_call x1, Pallas kernels, on_device(): pl.pallas_call(kernel, out_shape=jax.ShapeDtypeStruct((TOK, MODEL), BF),...  126 us
    unnamed x3, local copies, waits for them, and re-layouts  4.39 us

profile of v2, /device:TPU:1, one launch (start us, length us, event | category | flops | bytes accessed | tf_op | source)
XLA Modules:
  0.0 130.3 jit_solution(4341556952107793820)
XLA Ops:
  0.0 1.4 %copy.12.ids_ref = s32[32,8]{1,0:T(8,128)} copy(s32[32,8]{0,1:T(8,128)} %param.18) | data formatting | bytes 2048 | tf_op args[7]
  1.4 1.4 %copy.13.gates_ref = f32[32,8]{1,0:T(8,128)} copy(f32[32,8]{0,1:T(8,128)} %param.19) | data formatting | bytes 2048 | tf_op args[8]
  2.7 125.9 %layer.1 = bf16[32,4096]{1,0:T(8,128)(2,1)} custom-call(bf16[128,1024]{1,0:T(8,128)(2,1)} %q_ref.1, bf16[128,128]{1,0:T(8,128)(2,1)} %k_ref.1, bf16[128,128]{1,0:T(8,128)(2,1)} %v_ref.1, s32[1,128]{1,0:T(1,128)} %doc_ref.1, bf16[1024,128]{1,0:T(8,128)(2,1)} %wo_ref.1, bf16[32,4096]{1,0:T(8,128)(2,1)} %res_ref.1, f32[1,4096]{1,0:T(1,128)} %bitcast.1, ...), custom_call_target="tpu_custom_call" | custom-call | tf_op jit(solution)/shard_map/layer/pallas_call | solution.py:446
  128.6 1.7 %copy.15 = bf16[32,4096]{1,0:T(8,128)(2,1)} copy(bf16[32,4096]{1,0:T(8,128)(2,1)} %layer.1) | data formatting | bytes 524288

commit v3 on v2

--- a/solution.py
+++ b/solution.py
@@ -77,14 +77,16 @@
 
 
 def kernel(
-    q_ref, k_ref, v_ref, doc_ref, wo_ref, res_ref, gain_ref, ids_ref, gates_ref, w1_hbm, w2_hbm, out_ref, *scratch
+    *refs
 ):
     n = len(CHUNKS)
+    operands, (w1_hbm, w2_hbm, out_ref), inputs, scratch = refs[:9], refs[9:12], refs[12:21], refs[21:]
+    q_ref, k_ref, v_ref, doc_ref, ids_ref, gates_ref, wo_ref, gain_ref, res_ref = inputs
     (w1, w2, b_buf, a_buf, c_send, c_recv, hid, proj, act, act_p, meta, turn, meta_all, sel, wgt, perm, perm_t) = scratch[:17]
     rest = scratch[17:]
     gath, slot_send, slot_recv, ret_recv, part, part_recv = (rest[i * n : (i + 1) * n] for i in range(6))
     (
-        w_sem, b_send_sem, b_recv_sem, b_sib_sem, a_send_sem, a_recv_sem, c_send_sem, c_recv_sem, m_send_sem, m_recv_sem,
+        in_sem, w_sem, b_send_sem, b_recv_sem, b_sib_sem, a_send_sem, a_recv_sem, c_send_sem, c_recv_sem, m_send_sem, m_recv_sem,
         g_send_sem, g_recv_sem, s_send_sem, s_recv_sem, y_send_sem, y_recv_sem, z_send_sem, z_recv_sem,
     ) = rest[6 * n :]
 
@@ -104,19 +106,63 @@
     def wait_bytes(ref, sem):
         pltpu.make_async_copy(ref, ref, sem).wait()
 
+    takes = [pltpu.make_async_copy(src, dst, in_sem.at[i]) for i, (src, dst) in enumerate(zip(operands, inputs))]
+    for copy in takes:
+        copy.start()
     barrier = pltpu.get_barrier_semaphore()
 
     def greet(to):
         pl.semaphore_signal(barrier, inc=1, device_id=device(*to))
         return 0
 
-    def moved(dx, dy, dz, dc):
-        return lax.rem(x + dx, 4), lax.rem(y + dy, 4), lax.rem(z + dz, 4), lax.rem(c + dc, 2)
-
-    lax.fori_loop(1, 32, lambda k, _: greet(moved(k // 8, 0, lax.rem(k // 2, 4), lax.rem(k, 2))), 0)
-    lax.fori_loop(8, 32, lambda k, _: greet(moved(0, k // 8, lax.rem(k // 2, 4), lax.rem(k, 2))), 0)
-    lax.fori_loop(6, 24, lambda k, _: greet(moved(k // 6, 1 + lax.rem(k // 2, 3), 0, lax.rem(k, 2))), 0)
-
+    lax.fori_loop(1, 4, lambda k, _: greet((lax.rem(x + k, 4), y, z, c)), 0)
+    greet((x, y, z, 1 - c))
+    lax.fori_loop(1, 16, lambda k, _: greet((x, lax.rem(y + k // 4, 4), lax.rem(z + k, 4), c)), 0)
+
+    for copy in takes[:6]:
+        copy.wait()
+    doc = jnp.broadcast_to(doc_ref[...].astype(F32), (128, 128))
+    visible = (doc == doc.T) & (iota((128, 128), 0) >= iota((128, 128), 1))
+    keys = k_ref[...]
+    vals = v_ref[...]
+
+    def attend(h):
+        query = q_ref[:, h * HEAD : (h + 1) * HEAD]
+        scores = lax.dot_general(query, keys, (((1,), (1,)), ((), ())), preferred_element_type=F32)
+        scores = jnp.where(visible, scores * (1.0 / HEAD**0.5), -1e30)
+        top = jnp.max(scores, axis=-1, keepdims=True)
+        expo = jnp.where(visible, jnp.exp(scores - top), 0.0)
+        weights = (expo / jnp.sum(expo, axis=-1, keepdims=True)).astype(BF)
+        a_buf[z, :, h * HEAD : (h + 1) * HEAD] = dot(weights, vals).astype(BF)
+
+    def send_heads(half):
+        cols = pl.ds(half * 512, 512)
+        for d in (1, 3):
+            to = (x, y, lax.rem(z + d, 4), c)
+            remote(a_buf.at[z, :, cols], a_buf.at[z, :, cols], a_send_sem, a_recv_sem.at[d - 1], to).start()
+
+    def b_cols(xx, cc):
+        return pl.ds(pl.multiple_of((xx * 2 + cc) * 128, 128), 128)
+
+    lanes = iota((8, 128), 1)
+    for i, ref in enumerate((ids_ref, gates_ref)):
+        turn[:, 0:TOK] = ref[...].astype(F32)
+        once = jnp.where(lanes < TOK, turn[...], 0.0)
+        meta[8 * i : 8 * i + 8] = once + sum(pltpu.roll(once, TOK * s, 1) for s in (1, 2, 3))
+    for h in range(4):
+        attend(h)
+    takes[6].wait()
+    pl.semaphore_wait(barrier, 19)
+    sibling = (x, y, z, 1 - c)
+    for a in range(3):
+        for d in (1, 3, 2):
+            to = line_partner(a, x, y, z, d) + (c,)
+            remote(meta, meta_all.at[a, along[a]], m_send_sem, m_recv_sem, to).start()
+    remote(wo_ref, b_buf.at[:, b_cols(x, c)], b_send_sem, b_sib_sem.at[0], sibling).start()
+    for d in (1, 3):
+        to = (lax.rem(x + d, 4), y, z, c)
+        remote(wo_ref, b_buf.at[:, b_cols(x, c)], b_send_sem, b_recv_sem.at[d - 1], to).start()
+    send_heads(0)
     loads = []
     for i in range(4):
         loads.append(
@@ -129,50 +175,6 @@
     for copy in loads:
         copy.start()
 
-    doc = jnp.broadcast_to(doc_ref[...].astype(F32), (128, 128))
-    visible = (doc == doc.T) & (iota((128, 128), 0) >= iota((128, 128), 1))
-    keys = k_ref[...]
-    vals = v_ref[...]
-
-    def attend(h):
-        query = q_ref[:, h * HEAD : (h + 1) * HEAD]
-        scores = lax.dot_general(query, keys, (((1,), (1,)), ((), ())), preferred_element_type=F32)
-        scores = jnp.where(visible, scores * (1.0 / HEAD**0.5), -1e30)
-        top = jnp.max(scores, axis=-1, keepdims=True)
-        expo = jnp.where(visible, jnp.exp(scores - top), 0.0)
-        weights = (expo / jnp.sum(expo, axis=-1, keepdims=True)).astype(BF)
-        a_buf[z, :, h * HEAD : (h + 1) * HEAD] = dot(weights, vals).astype(BF)
-
-    def send_heads(half):
-        cols = pl.ds(half * 512, 512)
-        for d in (1, 3, 2):
-            to = (x, y, lax.rem(z + d, 4), c)
-            remote(a_buf.at[z, :, cols], a_buf.at[z, :, cols], a_send_sem, a_recv_sem.at[d - 1], to).start()
-
-    def b_cols(xx, cc):
-        return pl.ds(pl.multiple_of((xx * 2 + cc) * 128, 128), 128)
-
-    for s in range(4):
-        turn[s * TOK : (s + 1) * TOK, 0:8] = ids_ref[...].astype(F32)
-    meta[0:8] = turn[...].T[0:8]
-    for s in range(4):
-        turn[s * TOK : (s + 1) * TOK, 0:8] = gates_ref[...]
-    meta[8:16] = turn[...].T[0:8]
-    for h in range(4):
-        attend(h)
-    pl.semaphore_wait(barrier, 73)
-    sibling = (x, y, z, 1 - c)
-    remote(wo_ref, b_buf.at[:, b_cols(x, c)], b_send_sem, b_sib_sem.at[0], sibling).start()
-    for d in (1, 3):
-        to = (lax.rem(x + d, 4), y, z, c)
-        remote(wo_ref, b_buf.at[:, b_cols(x, c)], b_send_sem, b_recv_sem.at[d - 1], to).start()
-    for a in range(3):
-        for d in (1, 3, 2):
-            to = line_partner(a, x, y, z, d) + (c,)
-            remote(meta, meta_all.at[a, along[a]], m_send_sem, m_recv_sem, to).start()
-    to = (lax.rem(x + 2, 4), y, z, c)
-    remote(wo_ref, b_buf.at[:, b_cols(x, c)], b_send_sem, b_recv_sem.at[1], to).start()
-    send_heads(0)
     for h in range(4, 8):
         attend(h)
     send_heads(1)
@@ -242,28 +244,34 @@
             block = b_buf.at[:, b_cols(xx, c)]
             wait_bytes(block, b_recv_sem.at[e - 1])
             remote(block, block, b_send_sem, b_sib_sem.at[e], sibling).start()
+        if e in (1, 3):
+            half = b_buf.at[pl.ds(0 if e == 1 else 512, 512), b_cols(xx, c)]
+            remote(half, half, b_send_sem, b_recv_sem.at[1], (lax.rem(x + e, 4), y, z, c)).start()
 
     def columns_ready(e):
         xx = lax.rem(x + 4 - e, 4)
         wait_bytes(b_buf.at[:, b_cols(xx, 1 - c)], b_sib_sem.at[e])
 
     def heads_ready(d):
-        wait_bytes(a_buf.at[lax.rem(z + 4 - d, 4)], a_recv_sem.at[d - 1])
+        zz = lax.rem(z + 4 - d, 4)
+        wait_bytes(a_buf.at[zz], a_recv_sem.at[d - 1])
+        if d in (1, 3):
+            half = a_buf.at[zz, :, pl.ds(0 if d == 1 else 512, 512)]
+            remote(half, half, a_send_sem, a_recv_sem.at[1], (x, y, lax.rem(z + d, 4), c)).start()
 
     columns_ready(0)
     project(0, 0)
     columns_in(1)
     columns_in(3)
+    heads_ready(1)
+    heads_ready(3)
     columns_ready(1)
-    project(0, 1)
     columns_ready(3)
-    project(0, 3)
-    heads_ready(1)
-    for e in (0, 1, 3):
-        project(1, e)
-    heads_ready(3)
-    for e in (0, 1, 3):
-        project(3, e)
+    for e in (1, 3):
+        project(0, e)
+    for d in (1, 3):
+        for e in (0, 1, 3):
+            project(d, e)
     columns_in(2)
     columns_ready(2)
     for d in (0, 1, 3):
@@ -272,6 +280,8 @@
     for e in (0, 1, 3, 2):
         project(2, e)
     wait_bytes(c_recv.at[pl.ds(0, 15)], c_recv_sem)
+    for copy in takes[7:]:
+        copy.wait()
     square = jnp.zeros((TOK, 256), F32)
     for zz in range(4):
         for xx in range(4):
@@ -291,33 +301,43 @@
             mine = gath[i].at[along[a]]
             remote(mine, mine, g_send_sem.at[i], g_recv_sem.at[i], to).start()
 
-    def exchange(members, sources, targets, send_sem, recv_sem):
+    def exchange(members, sources, targets, send_sem, recv_sem, core):
+        def put(i, to):
+            a = CHUNKS[i][0]
+            remote(
+                sources[i].at[plane_index(a, *to)],
+                targets[i].at[plane_index(a, *me)],
+                send_sem.at[i],
+                recv_sem.at[i],
+                to,
+            ).start()
+
         def step(k, _):
             for i in members:
-                a = CHUNKS[i][0]
-                to = plane_partner(a, *me, k)
-                remote(
-                    sources[i].at[plane_index(a, *to)],
-                    targets[i].at[plane_index(a, *me)],
-                    send_sem.at[i],
-                    recv_sem.at[i],
-                    to,
-                ).start()
+                px, py, pz, _c = plane_partner(CHUNKS[i][0], x, y, z, c, k * 2)
+                put(i, (px, py, pz, core))
             return 0
 
-        lax.fori_loop(1, 32, step, 0)
-        for i in members:
-            mine = plane_index(CHUNKS[i][0], *me)
-            targets[i][mine] = sources[i][mine]
+        lax.fori_loop(1, 16, step, 0)
+        if core == 0:
+            for i in members:
+                put(i, sibling)
+                mine = plane_index(CHUNKS[i][0], *me)
+                targets[i][mine] = sources[i][mine]
 
     for group in range(GROUPS):
+        for i in range(n):
+            if CHUNKS[i][3] == group:
+                wait_bytes(gath[i].at[pl.ds(0, 3)], g_recv_sem.at[i])
         for i, (a, col, width, grp) in enumerate(CHUNKS):
             if grp == group:
-                wait_bytes(gath[i].at[pl.ds(0, 3)], g_recv_sem.at[i])
                 rows = dot(sel[a], gath[i][...].reshape(128, width))
                 slot_send[i][...] = rows.astype(BF).reshape(32, 16, width)
         members = [i for i in range(n) if CHUNKS[i][3] == group]
-        exchange(members, slot_send, slot_recv, s_send_sem, s_recv_sem)
+        exchange(members, slot_send, slot_recv, s_send_sem, s_recv_sem, 0)
+    for group in range(GROUPS):
+        members = [i for i in range(n) if CHUNKS[i][3] == group]
+        exchange(members, slot_send, slot_recv, s_send_sem, s_recv_sem, 1)
 
     for copy in loads:
         copy.wait()
@@ -333,24 +353,30 @@
                     moved = dot(perm[a // 2], block).astype(BF)
                     slot_recv[i][half * 16 : half * 16 + 16] = moved.reshape(16, 16, width)
 
-        def up(t, _, members=members, group=group):
-            cols = pl.ds(pl.multiple_of(t * 256, 256), 256)
+        def gather_up(cols, members=members, group=group):
             total = proj[:, cols] if group else jnp.zeros((512, 256), F32)
             for i in members:
                 _, col, width, _ = CHUNKS[i]
                 total = total + dot(slot_recv[i][...].reshape(512, width), w1[col : col + width, cols])
-            proj[:, cols] = total
+            return total
+
+        def up(t, _, gather_up=gather_up):
+            cols = pl.ds(pl.multiple_of(t * 256, 256), 256)
+            proj[:, cols] = gather_up(cols)
             return 0
 
-        lax.fori_loop(0, 6, up, 0)
-
-    def activate(t, _):
-        rows = pl.ds(pl.multiple_of(t * 64, 64), 64)
-        gate = proj[rows, :FF]
-        act[rows, :] = (gate / (1.0 + jnp.exp(-gate)) * proj[rows, FF:]).astype(BF)
-        return 0
-
-    lax.fori_loop(0, 8, activate, 0)
+        def last(t, _, gather_up=gather_up):
+            first = pl.multiple_of(t * 256, 256)
+            gate = gather_up(pl.ds(first, 256))
+            value = gather_up(pl.ds(pl.multiple_of(first + FF, 256), 256))
+            act[:, pl.ds(first, 256)] = (gate / (1.0 + jnp.exp(-gate)) * value).astype(BF)
+            return 0
+
+        if group < GROUPS - 1:
+            lax.fori_loop(0, 6, up, 0)
+        else:
+            lax.fori_loop(0, 3, last, 0)
+
     for i in range(2):
         for half in range(2):
             rows = slice(half * 256, half * 256 + 256)
@@ -362,7 +388,8 @@
             mine = act[...] if a == 1 else act_p[a // 2]
             rows = dot(mine, w2[:, col + t : col + t + 256]).astype(BF)
             slot_send[i][:, :, t : t + 256] = rows.reshape(32, 16, 256)
-        exchange([i], slot_send, ret_recv, y_send_sem, y_recv_sem)
+        for core in range(2):
+            exchange([i], slot_send, ret_recv, y_send_sem, y_recv_sem, core)
 
     for group in range(GROUPS):
         for i, (a, col, width, grp) in enumerate(CHUNKS):
@@ -415,7 +442,11 @@
         return pltpu.VMEM(shape, dtype)
 
     widths = [chunk[2] for chunk in CHUNKS]
-    scratch = [
+    operands = (
+        queries, keys, values, document_index, expert_ids.T, gate_weights.T, out_proj, norm_gain.reshape(1, -1), residual_in
+    )
+    scratch = [pltpu.VMEM(value.shape, value.dtype) for value in operands]
+    scratch += [
         buf(MODEL, 2 * FF),
         buf(FF, MODEL),
         buf(1024, 1024),
@@ -427,7 +458,7 @@
         buf(512, FF),
         buf(2, 512, FF),
         buf(16, 128, dtype=F32),
-        buf(128, 128, dtype=F32),
+        buf(8, 128, dtype=F32),
         buf(3, 4, 16, 128, dtype=F32),
         buf(3, 512, 128),
         buf(3, 256, 512),
@@ -440,23 +471,21 @@
     for _ in range(2):
         scratch += [buf(4, TOK, w) for w in widths]
     scratch += [
-        dma((6,)), dma, dma((3,)), dma((4,)), dma, dma((3,)), dma, dma, dma, dma,
+        dma((9,)), dma((6,)), dma, dma((3,)), dma((4,)), dma, dma((3,)), dma, dma, dma, dma,
         dma((n,)), dma((n,)), dma((n,)), dma((n,)), dma((n,)), dma((n,)), dma((n,)), dma((n,)),
     ]
-    return pl.pallas_call(
+    out = pl.pallas_call(
         kernel,
         out_shape=jax.ShapeDtypeStruct((TOK, MODEL), BF),
-        in_specs=[vmem] * 9 + [hbm] * 2,
+        in_specs=[hbm] * 11,
         out_specs=vmem,
         scratch_shapes=scratch,
         name="layer",
         compiler_params=pltpu.CompilerParams(
-            collective_id=0, has_side_effects=True, vmem_limit_bytes=66_000_000
+            collective_id=0, has_side_effects=True, vmem_limit_bytes=60_000_000
         ),
-    )(
-        queries, keys, values, document_index, out_proj, residual_in, norm_gain.reshape(1, -1), expert_ids, gate_weights,
-        w_gate_up, w_down
-    )
+    )(*operands, w_gate_up, w_down)
+    return out
 
 
 def solution(mesh):

time: 130 us -> 113 us (0.87)
  Pallas kernels: 126 us -> 111 us
  local copies, waits for them, and re-layouts: 4.39 us -> 1.67 us
    pallas_call x1, Pallas kernels: 126 us -> 111 us  [on_device(): pl.pallas_call(kernel, out_shape=jax.ShapeDtypeStruct((TOK, MODEL), BF),...]
    unnamed x3 -> x1, local copies, waits for them, and re-layouts: 4.39 us -> 1.67 us
where the time goes in v3:
time: 113 us
  Pallas kernels  111 us (98%)
  local copies, waits for them, and re-layouts  1.67 us (1%)
    pallas_call x1, Pallas kernels, on_device(): pl.pallas_call(kernel, out_shape=jax.ShapeDtypeStruct((TOK, MODEL), BF),...  111 us

profile of v3, /device:TPU:1, one launch (start us, length us, event | category | flops | bytes accessed | tf_op | source)
XLA Modules:
  0.0 112.9 jit_solution(493723769333605333)
XLA Ops:
  0.0 111.2 %layer.1 = bf16[32,4096]{1,0:T(8,128)(2,1)} custom-call(bf16[128,1024]{1,0:T(8,128)(2,1)} %refs_0_.1, bf16[128,128]{1,0:T(8,128)(2,1)} %refs_1_.1, bf16[128,128]{1,0:T(8,128)(2,1)} %refs_2_.1, s32[1,128]{1,0:T(1,128)} %refs_3_.1, s32[8,32]{1,0:T(8,128)} %bitcast.4, f32[8,32]{1,0:T(8,128)} %bitcast.5, bf16[1024,128]{1,0:T(8,128)(2,1)} %refs_6_.1, ...), custom_call_target="tpu_custom_call" | custom-call | tf_op jit(solution)/shard_map/layer/pallas_call | solution.py:477
  111.2 1.7 %copy.13 = bf16[32,4096]{1,0:T(8,128)(2,1)} copy(bf16[32,4096]{1,0:T(8,128)(2,1)} %layer.1) | data formatting | bytes 524288

commit v4 on v3

--- a/solution.py
+++ b/solution.py
@@ -86,7 +86,7 @@
     rest = scratch[17:]
     gath, slot_send, slot_recv, ret_recv, part, part_recv = (rest[i * n : (i + 1) * n] for i in range(6))
     (
-        in_sem, w_sem, b_send_sem, b_recv_sem, b_sib_sem, a_send_sem, a_recv_sem, c_send_sem, c_recv_sem, m_send_sem, m_recv_sem,
+        turn_sem, in_sem, w_sem, b_send_sem, b_recv_sem, b_sib_sem, a_send_sem, a_recv_sem, c_send_sem, c_recv_sem, m_send_sem, m_recv_sem,
         g_send_sem, g_recv_sem, s_send_sem, s_recv_sem, y_send_sem, y_recv_sem, z_send_sem, z_recv_sem,
     ) = rest[6 * n :]
 
@@ -135,11 +135,10 @@
         weights = (expo / jnp.sum(expo, axis=-1, keepdims=True)).astype(BF)
         a_buf[z, :, h * HEAD : (h + 1) * HEAD] = dot(weights, vals).astype(BF)
 
-    def send_heads(half):
-        cols = pl.ds(half * 512, 512)
-        for d in (1, 3):
-            to = (x, y, lax.rem(z + d, 4), c)
-            remote(a_buf.at[z, :, cols], a_buf.at[z, :, cols], a_send_sem, a_recv_sem.at[d - 1], to).start()
+    def send_heads(d, pair):
+        cols = pl.ds(pair * 256, 256)
+        to = (x, y, lax.rem(z + d, 4), c)
+        remote(a_buf.at[z, :, cols], a_buf.at[z, :, cols], a_send_sem, a_recv_sem.at[d - 1, pair], to).start()
 
     def b_cols(xx, cc):
         return pl.ds(pl.multiple_of((xx * 2 + cc) * 128, 128), 128)
@@ -149,7 +148,7 @@
         turn[:, 0:TOK] = ref[...].astype(F32)
         once = jnp.where(lanes < TOK, turn[...], 0.0)
         meta[8 * i : 8 * i + 8] = once + sum(pltpu.roll(once, TOK * s, 1) for s in (1, 2, 3))
-    for h in range(4):
+    for h in range(2):
         attend(h)
     takes[6].wait()
     pl.semaphore_wait(barrier, 19)
@@ -159,10 +158,19 @@
             to = line_partner(a, x, y, z, d) + (c,)
             remote(meta, meta_all.at[a, along[a]], m_send_sem, m_recv_sem, to).start()
     remote(wo_ref, b_buf.at[:, b_cols(x, c)], b_send_sem, b_sib_sem.at[0], sibling).start()
-    for d in (1, 3):
-        to = (lax.rem(x + d, 4), y, z, c)
-        remote(wo_ref, b_buf.at[:, b_cols(x, c)], b_send_sem, b_recv_sem.at[d - 1], to).start()
-    send_heads(0)
+    for d, halves in ((1, (0, 1)), (3, (1, 0))):
+        for half in halves:
+            rows = pl.ds(half * 512, 512)
+            to = (lax.rem(x + d, 4), y, z, c)
+            remote(
+                wo_ref.at[rows, :], b_buf.at[rows, b_cols(x, c)], b_send_sem, b_recv_sem.at[d - 1, half], to
+            ).start()
+
+    @pl.when(c == 0)
+    def _():
+        send_heads(1, 0)
+        send_heads(3, 0)
+
     loads = []
     for i in range(4):
         loads.append(
@@ -175,9 +183,26 @@
     for copy in loads:
         copy.start()
 
-    for h in range(4, 8):
-        attend(h)
-    send_heads(1)
+    for pair in range(1, 4):
+        for h in (2 * pair, 2 * pair + 1):
+            attend(h)
+
+        @pl.when(c == 0)
+        def _(pair=pair):
+            send_heads(1, pair)
+            if pair > 1:
+                send_heads(3, pair)
+
+    @pl.when(c == 0)
+    def _():
+        send_heads(3, 1)
+
+    @pl.when(c == 1)
+    def _():
+        for up, down in ((0, 2), (1, 3), (2, 0), (3, 1)):
+            send_heads(1, up)
+            send_heads(3, down)
+
     b_buf[:, b_cols(x, c)] = wo_ref[...]
 
     for a in range(3):
@@ -223,62 +248,97 @@
         wgt[a, 0:128] = jnp.where(match, dot(pick, gate_hi), 0.0).T.astype(BF)
         wgt[a, 128:256] = jnp.where(match, dot(pick, gate_lo), 0.0).T.astype(BF)
 
-    def project(d, e):
-        zz = lax.rem(z + 4 - d, 4)
-        xx = lax.rem(x + 4 - e, 4)
-        cols = pl.ds(pl.multiple_of(xx * 256, 256), 256)
-        c_send[zz, :, cols] = dot(a_buf[zz], b_buf[:, cols]).astype(BF)
-        for dy in (1, 3, 2, 0):
+    def project(*blocks):
+        places = []
+        for d, e in blocks:
+            zz = lax.rem(z + 4 - d, 4)
+            xx = lax.rem(x + 4 - e, 4)
+            cols = pl.ds(pl.multiple_of(xx * 256, 256), 256)
+            c_send[zz, :, cols] = dot(a_buf[zz], b_buf[:, cols]).astype(BF)
+            places.append((d, zz, cols))
+        for dy in (1, 3, 0, 2):
             yy = lax.rem(y + dy, 4)
             rows = pl.ds(pl.multiple_of(yy * TOK, TOK), TOK)
-            if d or dy:
-                remote(
-                    c_send.at[zz, rows, cols], c_recv.at[y * 4 + z, :, cols], c_send_sem, c_recv_sem, (x, yy, zz, c)
-                ).start()
-            else:
-                c_recv[y * 4 + z, :, cols] = c_send[zz, rows, cols]
+            for d, zz, cols in places:
+                if d or dy:
+                    remote(
+                        c_send.at[zz, rows, cols], c_recv.at[y * 4 + z, :, cols], c_send_sem, c_recv_sem, (x, yy, zz, c)
+                    ).start()
+                else:
+                    c_recv[y * 4 + z, :, cols] = c_send[zz, rows, cols]
+
+    def columns_half(e, half):
+        piece = b_buf.at[pl.ds(half * 512, 512), b_cols(lax.rem(x + 4 - e, 4), c)]
+        wait_bytes(piece, b_recv_sem.at[e - 1, half])
+        return piece
+
+    def columns_pass(e, half):
+        piece = columns_half(e, half)
+        remote(piece, piece, b_send_sem, b_recv_sem.at[1, half], (lax.rem(x + e, 4), y, z, c)).start()
 
     def columns_in(e):
-        xx = lax.rem(x + 4 - e, 4)
-        if e:
-            block = b_buf.at[:, b_cols(xx, c)]
-            wait_bytes(block, b_recv_sem.at[e - 1])
-            remote(block, block, b_send_sem, b_sib_sem.at[e], sibling).start()
-        if e in (1, 3):
-            half = b_buf.at[pl.ds(0 if e == 1 else 512, 512), b_cols(xx, c)]
-            remote(half, half, b_send_sem, b_recv_sem.at[1], (lax.rem(x + e, 4), y, z, c)).start()
+        block = b_buf.at[:, b_cols(lax.rem(x + 4 - e, 4), c)]
+        remote(block, block, b_send_sem, b_sib_sem.at[e], sibling).start()
 
     def columns_ready(e):
         xx = lax.rem(x + 4 - e, 4)
         wait_bytes(b_buf.at[:, b_cols(xx, 1 - c)], b_sib_sem.at[e])
 
-    def heads_ready(d):
-        zz = lax.rem(z + 4 - d, 4)
-        wait_bytes(a_buf.at[zz], a_recv_sem.at[d - 1])
-        if d in (1, 3):
-            half = a_buf.at[zz, :, pl.ds(0 if d == 1 else 512, 512)]
-            remote(half, half, a_send_sem, a_recv_sem.at[1], (x, y, lax.rem(z + d, 4), c)).start()
-
+    def heads_ready(d, pair):
+        piece = a_buf.at[lax.rem(z + 4 - d, 4), :, pl.ds(pair * 256, 256)]
+        wait_bytes(piece, a_recv_sem.at[d - 1, pair])
+        return piece
+
+    def heads_pass(d, pair):
+        piece = heads_ready(d, pair)
+        to = (x, y, lax.rem(z + d, 4), c)
+        remote(piece, piece, a_send_sem, a_recv_sem.at[1, pair], to).start()
+
+    heads_pass(1, 0)
+    columns_pass(1, 0)
+    columns_pass(3, 1)
+    heads_pass(1, 1)
     columns_ready(0)
-    project(0, 0)
+    project((0, 0))
+    heads_pass(3, 2)
+    heads_pass(3, 3)
+    columns_half(1, 1)
     columns_in(1)
+    columns_half(3, 0)
     columns_in(3)
-    heads_ready(1)
-    heads_ready(3)
+    for pair in (2, 3):
+        heads_ready(1, pair)
+    for pair in (0, 1):
+        heads_ready(3, pair)
     columns_ready(1)
     columns_ready(3)
-    for e in (1, 3):
-        project(0, e)
-    for d in (1, 3):
-        for e in (0, 1, 3):
-            project(d, e)
-    columns_in(2)
+
+    def far_columns():
+        columns_half(2, 0)
+        columns_half(2, 1)
+        columns_in(2)
+
+    @pl.when(c == 1)
+    def _():
+        far_columns()
+        pl.semaphore_wait(turn_sem, 1)
+
+    for e in (0, 1, 3):
+        project((1, e), (3, e), (0, e)) if e else project((1, e), (3, e))
+
+    @pl.when(c == 0)
+    def _():
+        pl.semaphore_signal(turn_sem, inc=1, device_id=device(*sibling))
+
+    @pl.when(c == 0)
+    def _():
+        far_columns()
+
+    for pair in range(4):
+        heads_ready(2, pair)
+    project((2, 0), (2, 1), (2, 3))
     columns_ready(2)
-    for d in (0, 1, 3):
-        project(d, 2)
-    heads_ready(2)
-    for e in (0, 1, 3, 2):
-        project(2, e)
+    project((2, 2), (1, 2), (3, 2), (0, 2))
     wait_bytes(c_recv.at[pl.ds(0, 15)], c_recv_sem)
     for copy in takes[7:]:
         copy.wait()
@@ -471,12 +531,12 @@
     for _ in range(2):
         scratch += [buf(4, TOK, w) for w in widths]
     scratch += [
-        dma((9,)), dma((6,)), dma, dma((3,)), dma((4,)), dma, dma((3,)), dma, dma, dma, dma,
+        pltpu.SemaphoreType.REGULAR, dma((9,)), dma((6,)), dma, dma((3, 2)), dma((4,)), dma, dma((3, 4)), dma, dma, dma, dma,
         dma((n,)), dma((n,)), dma((n,)), dma((n,)), dma((n,)), dma((n,)), dma((n,)), dma((n,)),
     ]
     out = pl.pallas_call(
         kernel,
-        out_shape=jax.ShapeDtypeStruct((TOK, MODEL), BF),
+        out_shape=pltpu.VMEM((TOK, MODEL), BF),
         in_specs=[hbm] * 11,
         out_specs=vmem,
         scratch_shapes=scratch,

time: 113 us -> 110 us (0.973)
  Pallas kernels: 111 us -> 109 us
    pallas_call x1, Pallas kernels: 111 us -> 109 us  [on_device(): pl.pallas_call(kernel, out_shape=pltpu.VMEM((TOK, MODEL), BF), in_specs=[...]
where the time goes in v4:
time: 110 us
  Pallas kernels  109 us (99%)
    pallas_call x1, Pallas kernels, on_device(): pl.pallas_call(kernel, out_shape=pltpu.VMEM((TOK, MODEL), BF), in_specs=[...  109 us

profile of v4, /device:TPU:1, one launch (start us, length us, event | category | flops | bytes accessed | tf_op | source)
XLA Modules:
  0.0 109.9 jit_solution(2340207467954717316)
XLA Ops:
  0.0 109.1 %layer.1 = bf16[32,4096]{1,0:T(8,128)(2,1)S(1)} custom-call(bf16[128,1024]{1,0:T(8,128)(2,1)} %refs_0_.1, bf16[128,128]{1,0:T(8,128)(2,1)} %refs_1_.1, bf16[128,128]{1,0:T(8,128)(2,1)} %refs_2_.1, s32[1,128]{1,0:T(1,128)} %refs_3_.1, s32[8,32]{1,0:T(8,128)} %bitcast.4, f32[8,32]{1,0:T(8,128)} %bitcast.5, bf16[1024,128]{1,0:T(8,128)(2,1)} %refs_6_.1, ...), custom_call_target="tpu_custom_call" | custom-call | tf_op jit(solution)/shard_map/layer/pallas_call | solution.py:537
  109.2 0.7 copy.13

commit v5 on v4

--- a/solution.py
+++ b/solution.py
@@ -374,7 +374,7 @@
 
         def step(k, _):
             for i in members:
-                px, py, pz, _c = plane_partner(CHUNKS[i][0], x, y, z, c, k * 2)
+                px, py, pz, _c = plane_partner(CHUNKS[i][0], x, y, z, c, lax.rem(k * 5, 16) * 2)
                 put(i, (px, py, pz, core))
             return 0
 
@@ -442,14 +442,17 @@
             rows = slice(half * 256, half * 256 + 256)
             act_p[i, rows, :] = dot(perm_t[i], act[rows, :]).astype(BF)
 
-    for i, (a, col, width, _) in enumerate(CHUNKS):
-        wait_bytes(slot_send[i].at[pl.ds(0, 31)], s_send_sem.at[i])
-        for t in range(0, width, 256):
-            mine = act[...] if a == 1 else act_p[a // 2]
-            rows = dot(mine, w2[:, col + t : col + t + 256]).astype(BF)
-            slot_send[i][:, :, t : t + 256] = rows.reshape(32, 16, 256)
+    for group in range(GROUPS):
+        for i, (a, col, width, grp) in enumerate(CHUNKS):
+            if grp == group:
+                wait_bytes(slot_send[i].at[pl.ds(0, 31)], s_send_sem.at[i])
+                for t in range(0, width, 256):
+                    mine = act[...] if a == 1 else act_p[a // 2]
+                    rows = dot(mine, w2[:, col + t : col + t + 256]).astype(BF)
+                    slot_send[i][:, :, t : t + 256] = rows.reshape(32, 16, 256)
+        members = [i for i in range(n) if CHUNKS[i][3] == group]
         for core in range(2):
-            exchange([i], slot_send, ret_recv, y_send_sem, y_recv_sem, core)
+            exchange(members, slot_send, ret_recv, y_send_sem, y_recv_sem, core)
 
     for group in range(GROUPS):
         for i, (a, col, width, grp) in enumerate(CHUNKS):

time: 110 us -> 109 us (level)
  no operation moved by 1% of the time
where the time goes in v5:
time: 109 us
  Pallas kernels  109 us (100%)
    pallas_call x1, Pallas kernels, on_device(): pl.pallas_call(kernel, out_shape=pltpu.VMEM((TOK, MODEL), BF), in_specs=[...  109 us

profile of v5, /device:TPU:1, one launch (start us, length us, event | category | flops | bytes accessed | tf_op | source)
XLA Modules:
  0.0 109.2 jit_solution(5989194866375473312)
XLA Ops:
  0.0 108.5 %layer.1 = bf16[32,4096]{1,0:T(8,128)(2,1)S(1)} custom-call(bf16[128,1024]{1,0:T(8,128)(2,1)} %refs_0_.1, bf16[128,128]{1,0:T(8,128)(2,1)} %refs_1_.1, bf16[128,128]{1,0:T(8,128)(2,1)} %refs_2_.1, s32[1,128]{1,0:T(1,128)} %refs_3_.1, s32[8,32]{1,0:T(8,128)} %bitcast.4, f32[8,32]{1,0:T(8,128)} %bitcast.5, bf16[1024,128]{1,0:T(8,128)(2,1)} %refs_6_.1, ...), custom_call_target="tpu_custom_call" | custom-call | tf_op jit(solution)/shard_map/layer/pallas_call | solution.py:540
  108.5 0.7 copy.13
